TPU v7x, 32 devices: a whole 2x2x4 slice. The times are simulated.
32 devices in a mesh: gx: 2 (over x), gy: 4 (over z), gz: 4 (over y, core).
Axes of the slice: x: 2, y: 2, z: 4, core: 2. Of those that a mesh axis runs over, the one named last changes fastest.
Arguments:
- pair_map: bfloat16 [160, 160, 128], P('gx', ('gy', 'gz')), may hold values from -6 to 6
- residue_mask: int32 [160], replicated, may hold values 0 or 1
- proj_weight: bfloat16 [128, 512], replicated, may hold values from -0.5 to 0.5
- gate_weight: bfloat16 [128, 128], replicated, may hold values from -0.5 to 0.5
- out_weight: bfloat16 [128, 128], replicated, may hold values from -0.5 to 0.5
Outputs:
- update: bfloat16 [160, 160, 128], P('gx', ('gy', 'gz'))
All inputs are finite; a program needn't handle non-finite values.
Results may differ from a plain program's by a relative error of at most 0.009.
Values may be sent and summed in bfloat16 or wider, within the bound.
A program may use at most 128 MiB of HBM per device.

v0:
```python
import jax
import jax.numpy as jnp
from jax import lax
from jax.sharding import PartitionSpec as P

epsilon = 1.0


def partner_2(x, axis, bit):
    return lax.ppermute(x, axis, [(i, i ^ 1 << bit) for i in range(lax.axis_size(axis))])


def layer_norm_lead(values):
    average = jnp.mean(values, axis=0, keepdims=True)
    centred = values - average
    variance = jnp.mean(centred * centred, axis=0, keepdims=True)
    return centred * lax.rsqrt(variance + epsilon)


def layer_norm_last(values):
    average = jnp.mean(values, axis=-1, keepdims=True)
    centred = values - average
    variance = jnp.mean(centred * centred, axis=-1, keepdims=True)
    return centred * lax.rsqrt(variance + epsilon)


def swap_with(values, bit):
    return partner_2(values, "gx", bit)


def pair_join(values, bit, position):
    partner = swap_with(values, bit)
    mine_first = position // 2**bit % 2 == 0
    return jnp.where(
        mine_first,
        jnp.concatenate([values, partner], axis=1),
        jnp.concatenate([partner, values], axis=1),
    )


def whole_channels(gathered, out_weight, gate_value):
    hidden, row_count, col_count = gathered.shape
    normed_tri = layer_norm_lead(gathered.astype(jnp.float32)).astype(jnp.bfloat16)
    mixed_out = lax.dot_general(
        normed_tri.reshape(hidden, row_count * col_count),
        out_weight,
        (((0,), (0,)), ((), ())),
        preferred_element_type=jnp.float32,
    )
    return gate_value * mixed_out.reshape(row_count, col_count, out_weight.shape[1])


def local(pair_map, residue_mask, proj_weight, gate_weight, out_weight):
    row_count, col_count, chan_count = pair_map.shape
    hidden = out_weight.shape[0]
    residues = residue_mask.shape[0]
    along_x = lax.axis_size("gx")
    along_y = lax.axis_size("gy")
    along_z = lax.axis_size("gz")
    mask_float = residue_mask.astype(jnp.float32)
    row_mask = lax.dynamic_slice_in_dim(mask_float, lax.axis_index("gx") * row_count, row_count)
    col_mask = lax.dynamic_slice_in_dim(
        mask_float, (lax.axis_index("gy") * along_z + lax.axis_index("gz")) * col_count, col_count
    )
    normed = layer_norm_last(pair_map.astype(jnp.float32)).astype(jnp.bfloat16)
    flattened = normed.reshape(row_count * col_count, chan_count)
    projected = lax.dot_general(
        proj_weight, flattened, (((0,), (1,)), ((), ())), preferred_element_type=jnp.float32
    ).reshape(4 * hidden, row_count, col_count)
    pair_mask = (row_mask[:, None] * col_mask[None, :])[None, :, :]
    left_proj = (
        jax.nn.sigmoid(projected[:hidden]) * projected[hidden : 2 * hidden] * pair_mask
    ).astype(jnp.bfloat16)
    right_proj = (
        jax.nn.sigmoid(projected[2 * hidden : 3 * hidden]) * projected[3 * hidden :] * pair_mask
    ).astype(jnp.bfloat16)
    gate_value = jax.nn.sigmoid(
        jnp.dot(flattened, gate_weight, preferred_element_type=jnp.float32)
    ).reshape(row_count, col_count, chan_count)
    group_count = along_y * along_z
    group_chan = hidden // group_count
    left_group, right_group = (
        lax.all_to_all(left_proj, ("gy", "gz"), split_axis=0, concat_axis=2, tiled=True),
        lax.all_to_all(right_proj, ("gy", "gz"), split_axis=0, concat_axis=2, tiled=True),
    )
    levels = along_x.bit_length() - 1
    low_bits = levels // 2
    high_count = 2 ** (levels - low_bits)
    low_count = 2**low_bits
    position = lax.axis_index("gx")
    left_tile = left_group
    for bit in range(low_bits):
        left_tile = pair_join(left_tile, bit, position)
    right_tile = right_group
    for bit in range(low_bits, levels):
        right_tile = pair_join(right_tile, bit, position)
    block_tile = jnp.einsum(
        "cik,cjk->cij", left_tile, right_tile, preferred_element_type=jnp.float32
    ).astype(jnp.bfloat16)
    for bit in range(low_bits):
        current = block_tile.shape[1]
        span = block_tile.shape[2]
        shaped = block_tile.reshape(group_chan, current // (2 * row_count), 2, row_count, span)
        own_bit = position // 2**bit % 2
        kept = lax.dynamic_index_in_dim(shaped, own_bit, axis=2, keepdims=False).reshape(
            group_chan, current // 2, span
        )
        sent = lax.dynamic_index_in_dim(shaped, 1 - own_bit, axis=2, keepdims=False).reshape(
            group_chan, current // 2, span
        )
        arrived = swap_with(sent, bit)
        block_tile = jnp.where(
            own_bit == 0,
            jnp.concatenate([kept, arrived], axis=2),
            jnp.concatenate([arrived, kept], axis=2),
        )
    block_tile = (
        block_tile.reshape(group_chan, row_count, low_count, high_count, row_count)
        .transpose(0, 1, 3, 2, 4)
        .reshape(group_chan, row_count, residues)
    )
    gathered = lax.all_to_all(block_tile, ("gy", "gz"), split_axis=2, concat_axis=0, tiled=True)
    update = whole_channels(gathered, out_weight, gate_value)
    return update.astype(jnp.bfloat16)


def solution(mesh):
    placed = (P("gx", ("gy", "gz"), None), P(), P(), P(), P())
    return jax.shard_map(
        local, mesh=mesh, in_specs=placed, out_specs=P("gx", ("gy", "gz"), None), check_vma=False
    )
```

profile of v0, /device:TPU:0, one launch (start us, length us, event | category | flops | bytes accessed | tf_op | source)
XLA Modules:
  0.0 66.7 jit_solution(2759295090196120318)
XLA Ops:
  0.0 0.7 %convert_element_type.46 = f32[160]{0:T(256)S(1)} convert(s32[160]{0:T(256)} %param.6) | non-fusion elementwise | flops 160 | bytes 1280 | tf_op jit(solution)/shard_map/convert_element_type | solution.py:60
  0.9 1.1 %convert_reduce_fusion = f32[80,10]{0,1:T(8,128)S(1)} fusion(bf16[80,10,128]{2,0,1:T(8,128)(2,1)} %param.5), kind=kLoop, calls=%fused_computation.15 | loop fusion | flops 204000 | bytes 208000 | tf_op jit(solution)/shard_map/reduce_sum | solution.py:21
  2.0 1.3 %fusion.7 = f32[80,10]{0,1:T(8,128)S(1)} fusion(bf16[80,10,128]{2,0,1:T(8,128)(2,1)} %param.5, f32[80,10]{0,1:T(8,128)S(1)} %broadcast_multiply_fusion.2), kind=kLoop, calls=%fused_computation.19 | loop fusion | flops 408800 | bytes 211200 | tf_op jit(solution)/shard_map/reduce_sum | solution.py:23
  3.3 1.2 %fusion.8 = bf16[80,10,128]{2,0,1:T(8,128)(2,1)S(1)} fusion(bf16[80,10,128]{2,0,1:T(8,128)(2,1)} %param.5, f32[80,10]{0,1:T(8,128)S(1)} %add_rsqrt_fusion.1, f32[80,10]{0,1:T(8,128)S(1)} %broadcast_multiply_fusion.2), kind=kLoop, calls=%fused_computation.20 | loop fusion | flops 409600 | bytes 416000 | tf_op jit(solution)/shard_map/convert_element_type | solution.py:65
  4.7 0.4 convolution_bitcast_fusion
  5.7 0.6 copy.45
  6.3 1.3 %reshape.105 = bf16[16,2,3200]{2,1,0:T(2,128)(2,1)} reshape(bf16[128,10,80]{2,1,0:T(8,128)(2,1)S(1)} %bitcast.40) | data formatting | bytes 409600
  7.6 7.4 %all-to-all-start.1 = ((bf16[16,2,3200]{2,1,0:T(2,128)(2,1)}), bf16[16,2,3200]{2,1,0:T(2,128)(2,1)S(1)}, u32[]{:S(2)}, u32[]{:S(2)}) async-start(bf16[16,2,3200]{2,1,0:T(2,128)(2,1)} %reshape.105), calls=%async_computation.1 | async-start | bytes 409600 | tf_op jit(solution)/shard_map/all_to_all | solution.py:84
  15.0 0.6 copy.42
  15.6 1.3 %reshape.107 = bf16[16,2,3200]{2,1,0:T(2,128)(2,1)} reshape(bf16[128,10,80]{2,1,0:T(8,128)(2,1)S(1)} %bitcast.41) | data formatting | bytes 409600
  16.8 7.3 %all-to-all-done.1 = bf16[16,2,3200]{2,1,0:T(2,128)(2,1)S(1)} async-done(((bf16[16,2,3200]{2,1,0:T(2,128)(2,1)}), bf16[16,2,3200]{2,1,0:T(2,128)(2,1)S(1)}, u32[]{:S(2)}, u32[]{:S(2)}) %all-to-all-start.1) | async-done | bytes 204832 | tf_op jit(solution)/shard_map/all_to_all | solution.py:84
  24.1 3.5 %all-to-all-start = ((bf16[16,2,3200]{2,1,0:T(2,128)(2,1)}), bf16[16,2,3200]{2,1,0:T(2,128)(2,1)S(1)}, u32[]{:S(2)}, u32[]{:S(2)}) async-start(bf16[16,2,3200]{2,1,0:T(2,128)(2,1)} %reshape.107), calls=%async_computation | async-start | bytes 409600 | tf_op jit(solution)/shard_map/all_to_all | solution.py:83
  27.6 0.6 reshape.106
  28.3 1.6 %collective-permute-start = (bf16[8,80,160]{1,0,2:T(8,128)(2,1)S(1)}, bf16[8,80,160]{1,0,2:T(8,128)(2,1)S(1)}, u32[]{:S(2)}, u32[]{:S(2)}) collective-permute-start(bf16[8,80,160]{1,0,2:T(8,128)(2,1)S(1)} %bitcast.45), channel_id=1, source_target_pairs={{0,16},{16,0},{1,17},{17,1},{2,18},{18,2},{3,19},{19,3},{4,20},{20... | collective-permute-start | bytes 614408 | tf_op jit(solution)/shard_map/ppermute | solution.py:10
  29.9 6.8 %all-to-all-done = bf16[16,2,3200]{2,1,0:T(2,128)(2,1)S(1)} async-done(((bf16[16,2,3200]{2,1,0:T(2,128)(2,1)}), bf16[16,2,3200]{2,1,0:T(2,128)(2,1)S(1)}, u32[]{:S(2)}, u32[]{:S(2)}) %all-to-all-start) | async-done | bytes 204832 | tf_op jit(solution)/shard_map/all_to_all | solution.py:83
  36.7 0.6 reshape.108
  37.4 0.9 %collective-permute-done = bf16[8,80,160]{1,0,2:T(8,128)(2,1)S(1)} collective-permute-done((bf16[8,80,160]{1,0,2:T(8,128)(2,1)S(1)}, bf16[8,80,160]{1,0,2:T(8,128)(2,1)S(1)}, u32[]{:S(2)}, u32[]{:S(2)}) %collective-permute-start) | collective-permute-done | bytes 204832 | tf_op jit(solution)/shard_map/ppermute | solution.py:10
  38.3 0.6 maximum_select_fusion
  39.2 0.9 %copy.50 = bf16[8,80,160]{1,0,2:T(8,128)(2,1)} copy(bf16[8,80,160]{2,1,0:T(8,128)(2,1)S(1)} %convolution_convert_fusion) | data formatting | bytes 409600 | tf_op jit(solution)/shard_map/convert_element_type | solution.py:99
  40.2 5.8 %all-to-all-start.2 = ((bf16[8,80,160]{1,0,2:T(8,128)(2,1)}), bf16[8,80,160]{1,0,2:T(8,128)(2,1)S(1)}, u32[]{:S(2)}, u32[]{:S(2)}) async-start(bf16[8,80,160]{1,0,2:T(8,128)(2,1)} %copy.50), calls=%async_computation.2 | async-start | bytes 655360 | tf_op jit(solution)/shard_map/all_to_all | solution.py:122
  46.3 10.7 %all-to-all-done.2 = bf16[8,80,160]{1,0,2:T(8,128)(2,1)S(1)} async-done(((bf16[8,80,160]{1,0,2:T(8,128)(2,1)}), bf16[8,80,160]{1,0,2:T(8,128)(2,1)S(1)}, u32[]{:S(2)}, u32[]{:S(2)}) %all-to-all-start.2) | async-done | bytes 204832 | tf_op jit(solution)/shard_map/all_to_all | solution.py:122
  57.7 3.2 %copy.51 = f32[16,8,80,10]{3,2,1,0:T(8,128)} copy(f32[16,8,80,10]{2,1,3,0:T(8,128)S(1)} %convert_bitcast_fusion) | data formatting | bytes 819200 | tf_op jit(solution)/shard_map/convert_element_type | solution.py:43
  60.9 4.2 %reshape.101 = f32[128,800]{1,0:T(8,128)S(1)} reshape(f32[16,8,80,10]{3,2,1,0:T(8,128)} %copy.51) | data formatting | bytes 819200 | tf_op jit(solution)/shard_map/convert_element_type | solution.py:43
  65.8 0.9 %fusion.3 = bf16[80,10,128]{2,0,1:T(8,128)(2,1)} fusion(f32[80,10,128]{2,1,0:T(8,128)S(1)} %reshape.98, bf16[80,10,128]{2,1,0:T(8,128)(2,1)S(1)} %dot_general.23, bf16[128,128]{1,0:T(8,128)(2,1)S(1)} %copy-done.1), kind=kOutput, calls=%fused_computation.7 | convolution fusion | flops 26419200 | bytes 851968 | tf_op jit(solution)/shard_map/dot_general | solution.py:44
  (34 shorter events, 3.1 us)
Async XLA Ops:
  0.0 4.7 %copy-start = (bf16[128,512]{1,0:T(8,128)(2,1)S(1)}, bf16[128,512]{1,0:T(8,128)(2,1)}, u32[]{:S(2)}) copy-start(bf16[128,512]{1,0:T(8,128)(2,1)} %param.7) | copy-start | bytes 393220
  7.6 16.5 %all-to-all-start.1 = ((bf16[16,2,3200]{2,1,0:T(2,128)(2,1)}), bf16[16,2,3200]{2,1,0:T(2,128)(2,1)S(1)}, u32[]{:S(2)}, u32[]{:S(2)}) async-start(bf16[16,2,3200]{2,1,0:T(2,128)(2,1)} %reshape.105), calls=%async_computation.1 | async-start | bytes 409600 | tf_op jit(solution)/shard_map/all_to_all | solution.py:84
  24.1 12.6 %all-to-all-start = ((bf16[16,2,3200]{2,1,0:T(2,128)(2,1)}), bf16[16,2,3200]{2,1,0:T(2,128)(2,1)S(1)}, u32[]{:S(2)}, u32[]{:S(2)}) async-start(bf16[16,2,3200]{2,1,0:T(2,128)(2,1)} %reshape.107), calls=%async_computation | async-start | bytes 409600 | tf_op jit(solution)/shard_map/all_to_all | solution.py:83
  28.3 10.0 %collective-permute-start = (bf16[8,80,160]{1,0,2:T(8,128)(2,1)S(1)}, bf16[8,80,160]{1,0,2:T(8,128)(2,1)S(1)}, u32[]{:S(2)}, u32[]{:S(2)}) collective-permute-start(bf16[8,80,160]{1,0,2:T(8,128)(2,1)S(1)} %bitcast.45), channel_id=1, source_target_pairs={{0,16},{16,0},{1,17},{17,1},{2,18},{18,2},{3,19},{19,3},{4,20},{20... | collective-permute-start | bytes 614408 | tf_op jit(solution)/shard_map/ppermute | solution.py:10
  38.9 7.1 %copy-start.2 = (bf16[128,128]{1,0:T(8,128)(2,1)S(1)}, bf16[128,128]{1,0:T(8,128)(2,1)}, u32[]{:S(2)}) copy-start(bf16[128,128]{1,0:T(8,128)(2,1)} %param.8) | copy-start | bytes 98308
  40.2 16.9 %all-to-all-start.2 = ((bf16[8,80,160]{1,0,2:T(8,128)(2,1)}), bf16[8,80,160]{1,0,2:T(8,128)(2,1)S(1)}, u32[]{:S(2)}, u32[]{:S(2)}) async-start(bf16[8,80,160]{1,0,2:T(8,128)(2,1)} %copy.50), calls=%async_computation.2 | async-start | bytes 655360 | tf_op jit(solution)/shard_map/all_to_all | solution.py:122
  65.1 0.8 %copy-start.1 = (bf16[128,128]{1,0:T(8,128)(2,1)S(1)}, bf16[128,128]{1,0:T(8,128)(2,1)}, u32[]{:S(2)}) copy-start(bf16[128,128]{1,0:T(8,128)(2,1)} %param.9) | copy-start | bytes 98308
where the time goes:
time: 67.3 us; the launch traced here: 66.7 us
  waiting for transfers between devices  25.7 us (38%)
  starting transfers between devices  18.3 us (27%)
  local copies, waits for them, and re-layouts  14.8 us (22%)
  other arithmetic  5.79 us (9%)
  matrix products  1.83 us (3%)
    all_to_all x1, waiting for transfers between devices, local(): lax.all_to_all(block_tile, ('gy', 'gz'), split_axis=2, concat_axis=0, til...  10.7 us
    all_to_all x1, starting transfers between devices, local(): lax.all_to_all(right_proj, ('gy', 'gz'), split_axis=0, concat_axis=2, til...  7.41 us
    convert_element_type x2, local copies, waits for them, and re-layouts, whole_channels(): gathered.astype(jnp.float32)  7.39 us
    all_to_all x1, waiting for transfers between devices, local(): lax.all_to_all(right_proj, ('gy', 'gz'), split_axis=0, concat_axis=2, til...  7.25 us
    all_to_all x1, waiting for transfers between devices, local(): lax.all_to_all(left_proj, ('gy', 'gz'), split_axis=0, concat_axis=2, tile...  6.78 us
    all_to_all x1, starting transfers between devices, local(): lax.all_to_all(block_tile, ('gy', 'gz'), split_axis=2, concat_axis=0, til...  5.8 us
    unnamed x10, local copies, waits for them, and re-layouts  4.06 us
    all_to_all x1, starting transfers between devices, local(): lax.all_to_all(left_proj, ('gy', 'gz'), split_axis=0, concat_axis=2, tile...  3.52 us
  transfers between devices with their start and end apart: 4, of which 4 were waited for; matrix products, arithmetic and copies ran while one was open for 5% of the time, Pallas kernels for 0%

commit v1 on v0

--- a/solution.py
+++ b/solution.py
@@ -1,6 +1,10 @@
+import functools
+
 import jax
 import jax.numpy as jnp
 from jax import lax
+from jax.experimental import pallas as pl
+from jax.experimental.pallas import tpu as pltpu
 from jax.sharding import PartitionSpec as P
 
 epsilon = 1.0
@@ -124,8 +128,267 @@
     return update.astype(jnp.bfloat16)
 
 
+MESH = pl.DeviceIdType.MESH
+LANES = 128
+VMEM_BUDGET = 48 * 2**20
+
+
+def up(value, step):
+    return -(-value // step) * step
+
+
+def fused_kernel(
+    along_y, along_z,
+    pair_ref, mask_ref, proj_ref, gate_ref, out_w_ref, out_ref,
+    rows_f32, normed_bf, masked_bf, gate_f32, send_a, recv_a, recv_x, left_s, right_s, tri_s, send_b, recv_b,
+    ssem_a, rsem_a, ssem_x, rsem_x, ssem_b, rsem_b, own_sem,
+):
+    rows, cols, chans = pair_ref.shape
+    hidden = out_w_ref.shape[0]
+    groups = along_y * along_z
+    gc = hidden // groups
+    pad = rows_f32.shape[0] // rows
+    flat = rows * cols
+    residues = mask_ref.shape[1]
+    px, py, pz = lax.axis_index("gx"), lax.axis_index("gy"), lax.axis_index("gz")
+    me = py * along_z + pz
+
+    def place(d):
+        return (px, d // along_z, d % along_z)
+
+    partner = (1 - px, py, pz)
+    barrier = pltpu.get_barrier_semaphore()
+
+    def greet(o, carry):
+        pl.semaphore_signal(barrier, inc=1, device_id=place((me + o) % groups), device_id_type=MESH)
+        return carry
+
+    lax.fori_loop(1, groups, greet, 0)
+    pl.semaphore_signal(barrier, inc=1, device_id=partner, device_id_type=MESH)
+
+    for i in range(rows):
+        rows_f32[pl.ds(i * pad, cols), :] = pair_ref[i].astype(jnp.float32)
+    mask_f = mask_ref[...].astype(jnp.float32)
+    lane = lax.broadcasted_iota(jnp.int32, (rows, residues), 1)
+    sub = lax.broadcasted_iota(jnp.int32, (rows, residues), 0)
+    row_mask = jnp.sum(jnp.where(lane == sub + px * rows, mask_f, 0.0), axis=1, keepdims=True)
+    lane_row = lax.broadcasted_iota(jnp.int32, (1, residues), 1)
+    for k in range(cols):
+        col_mask = jnp.sum(
+            jnp.where(lane_row == me * cols + k, mask_f, 0.0), axis=1, keepdims=True
+        )
+        normed = layer_norm_last(rows_f32[pl.ds(k, rows, stride=pad), :]).astype(jnp.bfloat16)
+        normed_bf[k * rows : (k + 1) * rows, :] = normed
+        masked_bf[k * rows : (k + 1) * rows, :] = (
+            normed.astype(jnp.float32) * (row_mask * col_mask)
+        ).astype(jnp.bfloat16)
+
+    proj_t = proj_ref[...].astype(jnp.float32).T.astype(jnp.bfloat16)
+    masked = masked_bf[...]
+
+    def project(first, count):
+        return lax.dot_general(
+            proj_t[first : first + count], masked, (((1,), (1,)), ((), ())),
+            preferred_element_type=jnp.float32,
+        )
+
+    step = 4 * gc
+    for first in range(0, hidden, step):
+        for side in range(2):
+            base = 2 * side * hidden + first
+            value = jax.nn.sigmoid(project(base, step)) * project(base + hidden, step)
+            for part in range(step // gc):
+                send_a[first // gc + part, side, :, 0:flat] = value[
+                    part * gc : (part + 1) * gc
+                ].astype(jnp.bfloat16)
+
+    def copy_a(d, slot):
+        return pltpu.make_async_remote_copy(
+            src_ref=send_a.at[d], dst_ref=recv_a.at[slot], send_sem=ssem_a.at[d],
+            recv_sem=rsem_a.at[slot], device_id=place(d), device_id_type=MESH,
+        )
+
+    def copy_x(s):
+        return pltpu.make_async_remote_copy(
+            src_ref=recv_a.at[s, 1], dst_ref=recv_x.at[s], send_sem=ssem_x.at[s],
+            recv_sem=rsem_x.at[s], device_id=partner, device_id_type=MESH,
+        )
+
+    def copy_b(d, slot):
+        return pltpu.make_async_remote_copy(
+            src_ref=send_b.at[d], dst_ref=recv_b.at[slot], send_sem=ssem_b.at[d],
+            recv_sem=rsem_b.at[slot], device_id=place(d), device_id_type=MESH,
+        )
+
+    pl.semaphore_wait(barrier, groups)
+
+    def start_a(o, carry):
+        copy_a((me + o) % groups, me).start()
+        return carry
+
+    lax.fori_loop(1, groups, start_a, 0)
+    own_a = pltpu.make_async_copy(send_a.at[me], recv_a.at[me], own_sem.at[0])
+    own_a.start()
+
+    gate_f32[...] = jax.nn.sigmoid(
+        jnp.dot(normed_bf[...], gate_ref[...], preferred_element_type=jnp.float32)
+    )
+
+    def spread(value, target, s):
+        value = value.astype(jnp.float32)
+        for k in range(cols):
+            at = pl.multiple_of((s * cols + k) * gc, gc)
+            target[pl.ds(at, gc), 0:rows] = value[:, k * rows : (k + 1) * rows]
+
+    def take(s):
+        copy_x(s).start()
+        spread(recv_a[s, 0], left_s, s)
+        spread(recv_a[s, 1], right_s.at[px], s)
+
+    own_a.wait()
+    take(me)
+
+    def take_a(o, carry):
+        s = (me + groups - o) % groups
+        copy_a(s, s).wait_recv()
+        take(s)
+        return carry
+
+    lax.fori_loop(1, groups, take_a, 0)
+
+    def take_x(o, carry):
+        s = (me + groups - o) % groups
+        copy_x(s).wait_recv()
+        spread(recv_x[s], right_s.at[1 - px], s)
+        return carry
+
+    lax.fori_loop(0, groups, take_x, 0)
+
+    for c in range(gc):
+        left = left_s[pl.ds(c, residues, stride=gc), :].astype(jnp.bfloat16)
+        for half in range(2):
+            right = right_s[half, pl.ds(c, residues, stride=gc), :].astype(jnp.bfloat16)
+            block = lax.dot_general(
+                right, left, (((0,), (0,)), ((), ())), preferred_element_type=jnp.float32
+            )
+            tri_s[pl.ds(half * rows * gc + c, rows, stride=gc), :] = block[0:rows]
+
+    def start_b(o, carry):
+        d = (me + o) % groups
+        pieces = []
+        for j in range(cols):
+            at = pl.multiple_of((d * cols + j) * gc, gc)
+            pieces.append(tri_s[pl.ds(at, gc), 0:rows])
+        send_b[d, :, 0:flat] = jnp.concatenate(pieces, axis=1).astype(jnp.bfloat16)
+
+        @pl.when(o < groups)
+        def _():
+            copy_b(d, me).start()
+
+        return carry
+
+    lax.fori_loop(1, groups + 1, start_b, 0)
+    own_b = pltpu.make_async_copy(send_b.at[me], recv_b.at[me], own_sem.at[1])
+    own_b.start()
+    own_b.wait()
+
+    def take_b(o, carry):
+        s = (me + groups - o) % groups
+        copy_b(s, s).wait_recv()
+        return carry
+
+    lax.fori_loop(1, groups, take_b, 0)
+
+    triangle = recv_b[:, :, 0:flat].astype(jnp.float32).reshape(hidden, flat)
+    normed_tri = layer_norm_lead(triangle).astype(jnp.bfloat16)
+    mixed = lax.dot_general(
+        normed_tri, out_w_ref[...], (((0,), (0,)), ((), ())), preferred_element_type=jnp.float32
+    )
+    update = gate_f32[...] * mixed
+    for j in range(cols):
+        rows_f32[pl.ds(j, rows, stride=pad), :] = update[j * rows : (j + 1) * rows]
+    for i in range(rows):
+        out_ref[i] = rows_f32[pl.ds(i * pad, cols), :].astype(jnp.bfloat16)
+
+    def finish(o, carry):
+        d = (me + o) % groups
+        copy_a(d, me).wait_send()
+        copy_b(d, me).wait_send()
+        return carry
+
+    lax.fori_loop(1, groups, finish, 0)
+
+    def finish_x(s, carry):
+        copy_x(s).wait_send()
+        return carry
+
+    lax.fori_loop(0, groups, finish_x, 0)
+
+
+def scratch_list(rows, cols, chans, hidden, groups, residues):
+    gc = hidden // groups
+    flat = up(rows * cols, LANES)
+    pad = up(cols, 8)
+    bf, f32 = jnp.bfloat16, jnp.float32
+    return [
+        ((rows * pad, chans), f32),
+        ((rows * cols, chans), bf),
+        ((rows * cols, chans), bf),
+        ((rows * cols, chans), f32),
+        ((groups, 2, gc, flat), bf),
+        ((groups, 2, gc, flat), bf),
+        ((groups, gc, flat), bf),
+        ((residues * gc, LANES), f32),
+        ((2, residues * gc, LANES), f32),
+        ((residues * gc, LANES), f32),
+        ((groups, gc, flat), bf),
+        ((groups, gc, flat), bf),
+    ]
+
+
+def fits_kernel(sizes, rows, cols, chans, hidden, residues):
+    groups = sizes["gy"] * sizes["gz"]
+    if sizes["gx"] != 2 or hidden % (4 * groups) or hidden // groups != 8:
+        return False
+    if chans != LANES or rows > LANES or rows % 16:
+        return False
+    total = 0
+    for shape, kind in scratch_list(rows, cols, chans, hidden, groups, residues):
+        count = 1
+        for extent in shape:
+            count *= extent
+        total += count * jnp.dtype(kind).itemsize
+    return total < VMEM_BUDGET // 4
+
+
+def local_fused(sizes, pair_map, residue_mask, proj_weight, gate_weight, out_weight):
+    rows, cols, chans = pair_map.shape
+    hidden = out_weight.shape[0]
+    residues = residue_mask.shape[0]
+    if not fits_kernel(sizes, rows, cols, chans, hidden, residues):
+        return local(pair_map, residue_mask, proj_weight, gate_weight, out_weight)
+    groups = sizes["gy"] * sizes["gz"]
+    dma = pltpu.SemaphoreType.DMA((groups,))
+    vmem = pl.BlockSpec(memory_space=pltpu.VMEM)
+    return pl.pallas_call(
+        functools.partial(fused_kernel, sizes["gy"], sizes["gz"]),
+        out_shape=jax.ShapeDtypeStruct(pair_map.shape, jnp.bfloat16),
+        in_specs=[vmem] * 5,
+        out_specs=vmem,
+        scratch_shapes=[
+            pltpu.VMEM(shape, kind)
+            for shape, kind in scratch_list(rows, cols, chans, hidden, groups, residues)
+        ]
+        + [dma] * 6
+        + [pltpu.SemaphoreType.DMA((2,))],
+        compiler_params=pltpu.CompilerParams(
+            collective_id=0, has_side_effects=True, vmem_limit_bytes=VMEM_BUDGET
+        ),
+    )(pair_map, residue_mask.reshape(1, residues), proj_weight, gate_weight, out_weight)
+
+
 def solution(mesh):
     placed = (P("gx", ("gy", "gz"), None), P(), P(), P(), P())
     return jax.shard_map(
-        local, mesh=mesh, in_specs=placed, out_specs=P("gx", ("gy", "gz"), None), check_vma=False
-    )
+        functools.partial(local_fused, dict(mesh.shape)), mesh=mesh, in_specs=placed, out_specs=P("gx", ("gy", "gz"), None), check_vma=False
+    )

time: 67.3 us -> 31.2 us (0.46)
  Pallas kernels: 0 us -> 29.2 us
  waiting for transfers between devices: 25.7 us -> 0 us
  starting transfers between devices: 18.3 us -> 0 us
  local copies, waits for them, and re-layouts: 14.8 us -> 1.79 us
  other arithmetic: 5.79 us -> 0 us
  matrix products: 1.83 us -> 0 us
    pallas_call x0 -> x1, Pallas kernels: none -> 29.2 us  [local_fused(): pl.pallas_call(functools.partial(fused_kernel, sizes['gy'], sizes['gz']),...]
    all_to_all x3 -> x0, waiting for transfers between devices: 24.8 us -> none  [the longest x1 10.7 us: local(): lax.all_to_all(block_tile, ('gy', 'gz'), split_axis=2, concat_axis=0, til...]
    all_to_all x3 -> x0, starting transfers between devices: 16.7 us -> none  [the longest x1 7.41 us: local(): lax.all_to_all(right_proj, ('gy', 'gz'), split_axis=0, concat_axis=2, til...]
    convert_element_type x6 -> x0, local copies, waits for them, and re-layouts: 9.54 us -> none  [the longest x2 7.39 us: whole_channels(): gathered.astype(jnp.float32)]
    unnamed x10 -> x9, local copies, waits for them, and re-layouts: 4.06 us -> 1.05 us
    reduce_sum x4 -> x0, other arithmetic: 2.63 us -> none  [the longest x1 1.32 us: layer_norm_last(): variance = jnp.mean(centred * centred, axis=-1, keepdims=True)]
    convert_element_type x4 -> x0, other arithmetic: 2.21 us -> none  [the longest x1 1.2 us: local(): normed = layer_norm_last(pair_map.astype(jnp.float32)).astype(jnp.bfloat16)]
    dot_general x4 -> x0, matrix products: 1.83 us -> none  [the longest x1 0.9 us: whole_channels(): lax.dot_general(normed_tri.reshape(hidden, row_count * col_count), out_we...]
  transfers between devices with their start and end apart: 4 -> 0, of which waited for: 4 -> 0; matrix products, arithmetic and copies ran while one was open for 5% -> 0% of each run, Pallas kernels for 0% -> 0%
where the time goes in v1:
time: 31.2 us; the launch traced here: 31 us
  Pallas kernels  29.2 us (94%)
  local copies, waits for them, and re-layouts  1.79 us (6%)
    pallas_call x1, Pallas kernels, local_fused(): pl.pallas_call(functools.partial(fused_kernel, sizes['gy'], sizes['gz']),...  29.2 us
    unnamed x9, local copies, waits for them, and re-layouts  1.05 us
    pallas_call x1, local copies, waits for them, and re-layouts, local_fused(): pl.pallas_call(functools.partial(fused_kernel, sizes['gy'], sizes['gz']),...  0.73 us

profile of v1, /device:TPU:0, one launch (start us, length us, event | category | flops | bytes accessed | tf_op | source)
XLA Modules:
  0.0 31.0 jit_solution(5592816732867006830)
XLA Ops:
  0.0 0.0 copy-start
  0.0 0.0 copy-start.1
  0.0 0.0 copy-start.2
  0.0 0.0 copy-start.3
  0.0 1.0 %copy.6.pair_ref = bf16[80,10,128]{2,1,0:T(8,128)(2,1)S(1)} copy(bf16[80,10,128]{2,0,1:T(8,128)(2,1)} %param.5) | data formatting | bytes 409600 | tf_op args[0]
  1.1 0.0 copy-done
  1.1 0.0 copy-done.1
  1.1 0.0 copy-done.2
  1.1 0.0 copy-done.3
  1.1 29.2 %shard_map.55 = bf16[80,10,128]{2,1,0:T(8,128)(2,1)S(1)} custom-call(bf16[80,10,128]{2,1,0:T(8,128)(2,1)S(1)} %copy.6.pair_ref, s32[1,160]{1,0:T(1,128)S(1)} %bitcast.1, bf16[128,512]{1,0:T(8,128)(2,1)S(1)} %copy-done, bf16[128,128]{1,0:T(8,128)(2,1)S(1)} %copy-done.1, bf16[128,128]{1,0:T(8,128)(2,1)S(1)} %copy-done.2), custom_call_target="tpu_custom_call" | custom-call | tf_op jit(solution)/shard_map/pallas_call | solution.py:373
  30.3 0.7 %copy.7 = bf16[80,10,128]{2,0,1:T(8,128)(2,1)} copy(bf16[80,10,128]{2,1,0:T(8,128)(2,1)S(1)} %shard_map.55) | data formatting | bytes 409600 | tf_op jit(solution)/shard_map/pallas_call | solution.py:373
Async XLA Ops:
  0.0 1.1 %copy-start = (bf16[128,512]{1,0:T(8,128)(2,1)S(1)}, bf16[128,512]{1,0:T(8,128)(2,1)}, u32[]{:S(2)}) copy-start(bf16[128,512]{1,0:T(8,128)(2,1)} %proj_ref.1) | copy-start | bytes 393220
  0.0 1.1 %copy-start.1 = (bf16[128,128]{1,0:T(8,128)(2,1)S(1)}, bf16[128,128]{1,0:T(8,128)(2,1)}, u32[]{:S(2)}) copy-start(bf16[128,128]{1,0:T(8,128)(2,1)} %gate_ref.1) | copy-start | bytes 98308
  0.0 1.1 %copy-start.2 = (bf16[128,128]{1,0:T(8,128)(2,1)S(1)}, bf16[128,128]{1,0:T(8,128)(2,1)}, u32[]{:S(2)}) copy-start(bf16[128,128]{1,0:T(8,128)(2,1)} %out_w_ref.1) | copy-start | bytes 98308
  0.0 1.1 %copy-start.3 = (s32[160]{0:T(256)S(1)}, s32[160]{0:T(256)}, u32[]{:S(2)}) copy-start(s32[160]{0:T(256)} %param.6) | copy-start | bytes 1924

commit v2 on v1

--- a/solution.py
+++ b/solution.py
@@ -140,14 +140,15 @@
 def fused_kernel(
     along_y, along_z,
     pair_ref, mask_ref, proj_ref, gate_ref, out_w_ref, out_ref,
-    rows_f32, normed_bf, masked_bf, gate_f32, send_a, recv_a, recv_x, left_s, right_s, tri_s, send_b, recv_b,
-    ssem_a, rsem_a, ssem_x, rsem_x, ssem_b, rsem_b, own_sem,
+    normed_bf, masked_bf, gate_f32, send_r, recv_r, recv_x, send_l, recv_l,
+    left_s, right_s, tri_s, send_b, recv_b,
+    ssem_r, rsem_r, ssem_x, rsem_x, ssem_l, rsem_l, ssem_b, rsem_b, own_sem,
 ):
-    rows, cols, chans = pair_ref.shape
+    cols, rows, chans = pair_ref.shape
     hidden = out_w_ref.shape[0]
     groups = along_y * along_z
     gc = hidden // groups
-    pad = rows_f32.shape[0] // rows
+    hc = gc // 2
     flat = rows * cols
     residues = mask_ref.shape[1]
     px, py, pz = lax.axis_index("gx"), lax.axis_index("gy"), lax.axis_index("gz")
@@ -166,8 +167,6 @@
     lax.fori_loop(1, groups, greet, 0)
     pl.semaphore_signal(barrier, inc=1, device_id=partner, device_id_type=MESH)
 
-    for i in range(rows):
-        rows_f32[pl.ds(i * pad, cols), :] = pair_ref[i].astype(jnp.float32)
     mask_f = mask_ref[...].astype(jnp.float32)
     lane = lax.broadcasted_iota(jnp.int32, (rows, residues), 1)
     sub = lax.broadcasted_iota(jnp.int32, (rows, residues), 0)
@@ -177,7 +176,7 @@
         col_mask = jnp.sum(
             jnp.where(lane_row == me * cols + k, mask_f, 0.0), axis=1, keepdims=True
         )
-        normed = layer_norm_last(rows_f32[pl.ds(k, rows, stride=pad), :]).astype(jnp.bfloat16)
+        normed = layer_norm_last(pair_ref[k].astype(jnp.float32)).astype(jnp.bfloat16)
         normed_bf[k * rows : (k + 1) * rows, :] = normed
         masked_bf[k * rows : (k + 1) * rows, :] = (
             normed.astype(jnp.float32) * (row_mask * col_mask)
@@ -192,128 +191,163 @@
             preferred_element_type=jnp.float32,
         )
 
-    step = 4 * gc
-    for first in range(0, hidden, step):
-        for side in range(2):
-            base = 2 * side * hidden + first
-            value = jax.nn.sigmoid(project(base, step)) * project(base + hidden, step)
-            for part in range(step // gc):
-                send_a[first // gc + part, side, :, 0:flat] = value[
-                    part * gc : (part + 1) * gc
-                ].astype(jnp.bfloat16)
-
-    def copy_a(d, slot):
+    def copy_r(d, slot):
         return pltpu.make_async_remote_copy(
-            src_ref=send_a.at[d], dst_ref=recv_a.at[slot], send_sem=ssem_a.at[d],
-            recv_sem=rsem_a.at[slot], device_id=place(d), device_id_type=MESH,
+            src_ref=send_r.at[d], dst_ref=recv_r.at[slot], send_sem=ssem_r.at[d],
+            recv_sem=rsem_r.at[slot], device_id=place(d), device_id_type=MESH,
+        )
+
+    def copy_l(h, d, slot):
+        return pltpu.make_async_remote_copy(
+            src_ref=send_l.at[h, d], dst_ref=recv_l.at[h, slot], send_sem=ssem_l.at[h, d],
+            recv_sem=rsem_l.at[h, slot], device_id=place(d), device_id_type=MESH,
         )
 
     def copy_x(s):
         return pltpu.make_async_remote_copy(
-            src_ref=recv_a.at[s, 1], dst_ref=recv_x.at[s], send_sem=ssem_x.at[s],
+            src_ref=recv_r.at[s], dst_ref=recv_x.at[s], send_sem=ssem_x.at[s],
             recv_sem=rsem_x.at[s], device_id=partner, device_id_type=MESH,
         )
 
-    def copy_b(d, slot):
+    def copy_b(h, d, slot):
         return pltpu.make_async_remote_copy(
-            src_ref=send_b.at[d], dst_ref=recv_b.at[slot], send_sem=ssem_b.at[d],
-            recv_sem=rsem_b.at[slot], device_id=place(d), device_id_type=MESH,
-        )
+            src_ref=send_b.at[h, d], dst_ref=recv_b.at[h, slot], send_sem=ssem_b.at[h, d],
+            recv_sem=rsem_b.at[h, slot], device_id=place(d), device_id_type=MESH,
+        )
+
+    step = 4 * gc
+
+    def gated(first, side):
+        base = 2 * side * hidden + first
+        return jax.nn.sigmoid(project(base, step)) * project(base + hidden, step)
+
+    for first in range(0, hidden, step):
+        value = gated(first, 1)
+        for part in range(step // gc):
+            send_r[first // gc + part, :, 0:flat] = value[
+                part * gc : (part + 1) * gc
+            ].astype(jnp.bfloat16)
 
     pl.semaphore_wait(barrier, groups)
 
-    def start_a(o, carry):
-        copy_a((me + o) % groups, me).start()
-        return carry
-
-    lax.fori_loop(1, groups, start_a, 0)
-    own_a = pltpu.make_async_copy(send_a.at[me], recv_a.at[me], own_sem.at[0])
-    own_a.start()
+    def start_r(o, carry):
+        copy_r((me + o) % groups, me).start()
+        return carry
+
+    lax.fori_loop(1, groups, start_r, 0)
+    own_r = pltpu.make_async_copy(send_r.at[me], recv_r.at[me], own_sem.at[0])
+    own_r.start()
+
+    for first in range(0, hidden, step):
+        value = gated(first, 0)
+        for part in range(step // gc):
+            for h in range(2):
+                low = part * gc + h * hc
+                send_l[h, first // gc + part, :, 0:flat] = value[low : low + hc].astype(jnp.bfloat16)
+
+    for h in range(2):
+
+        def start_l(o, carry, h=h):
+            copy_l(h, (me + o) % groups, me).start()
+            return carry
+
+        lax.fori_loop(1, groups, start_l, 0)
 
     gate_f32[...] = jax.nn.sigmoid(
         jnp.dot(normed_bf[...], gate_ref[...], preferred_element_type=jnp.float32)
     )
 
-    def spread(value, target, s):
+    def spread(value, target, s, first, count):
         value = value.astype(jnp.float32)
         for k in range(cols):
             at = pl.multiple_of((s * cols + k) * gc, gc)
-            target[pl.ds(at, gc), 0:rows] = value[:, k * rows : (k + 1) * rows]
-
-    def take(s):
+            target[pl.ds(at + first, count), 0:rows] = value[:, k * rows : (k + 1) * rows]
+
+    own_r.wait()
+
+    def take_r(o, carry):
+        s = (me + groups - o) % groups
+
+        @pl.when(o > 0)
+        def _():
+            copy_r(s, s).wait_recv()
+
         copy_x(s).start()
-        spread(recv_a[s, 0], left_s, s)
-        spread(recv_a[s, 1], right_s.at[px], s)
-
-    own_a.wait()
-    take(me)
-
-    def take_a(o, carry):
-        s = (me + groups - o) % groups
-        copy_a(s, s).wait_recv()
-        take(s)
-        return carry
-
-    lax.fori_loop(1, groups, take_a, 0)
+        spread(recv_r[s], right_s.at[px], s, 0, gc)
+        return carry
+
+    lax.fori_loop(0, groups, take_r, 0)
 
     def take_x(o, carry):
         s = (me + groups - o) % groups
         copy_x(s).wait_recv()
-        spread(recv_x[s], right_s.at[1 - px], s)
+        spread(recv_x[s], right_s.at[1 - px], s, 0, gc)
         return carry
 
     lax.fori_loop(0, groups, take_x, 0)
 
-    for c in range(gc):
-        left = left_s[pl.ds(c, residues, stride=gc), :].astype(jnp.bfloat16)
-        for half in range(2):
-            right = right_s[half, pl.ds(c, residues, stride=gc), :].astype(jnp.bfloat16)
-            block = lax.dot_general(
-                right, left, (((0,), (0,)), ((), ())), preferred_element_type=jnp.float32
-            )
-            tri_s[pl.ds(half * rows * gc + c, rows, stride=gc), :] = block[0:rows]
-
-    def start_b(o, carry):
-        d = (me + o) % groups
-        pieces = []
-        for j in range(cols):
-            at = pl.multiple_of((d * cols + j) * gc, gc)
-            pieces.append(tri_s[pl.ds(at, gc), 0:rows])
-        send_b[d, :, 0:flat] = jnp.concatenate(pieces, axis=1).astype(jnp.bfloat16)
-
-        @pl.when(o < groups)
-        def _():
-            copy_b(d, me).start()
-
-        return carry
-
-    lax.fori_loop(1, groups + 1, start_b, 0)
-    own_b = pltpu.make_async_copy(send_b.at[me], recv_b.at[me], own_sem.at[1])
-    own_b.start()
-    own_b.wait()
-
-    def take_b(o, carry):
-        s = (me + groups - o) % groups
-        copy_b(s, s).wait_recv()
-        return carry
-
-    lax.fori_loop(1, groups, take_b, 0)
-
-    triangle = recv_b[:, :, 0:flat].astype(jnp.float32).reshape(hidden, flat)
+    for h in range(2):
+        spread(send_l[h, me], left_s, me, h * hc, hc)
+
+        def take_l(o, carry, h=h):
+            s = (me + groups - o) % groups
+            copy_l(h, s, s).wait_recv()
+            spread(recv_l[h, s], left_s, s, h * hc, hc)
+            return carry
+
+        lax.fori_loop(1, groups, take_l, 0)
+
+        for c in range(h * hc, (h + 1) * hc):
+            left = left_s[pl.ds(c, residues, stride=gc), :].astype(jnp.bfloat16)
+            for half in range(2):
+                right = right_s[half, pl.ds(c, residues, stride=gc), :].astype(jnp.bfloat16)
+                block = lax.dot_general(
+                    right, left, (((0,), (0,)), ((), ())), preferred_element_type=jnp.float32
+                )
+                tri_s[pl.ds(half * rows * gc + c, rows, stride=gc), :] = block[0:rows]
+
+        def pack_b(d, h=h):
+            pieces = []
+            for j in range(cols):
+                at = pl.multiple_of((d * cols + j) * gc, gc)
+                pieces.append(tri_s[pl.ds(at + h * hc, hc), 0:rows])
+            return jnp.concatenate(pieces, axis=1).astype(jnp.bfloat16)
+
+        def start_b(o, carry, h=h):
+            d = (me + o) % groups
+            send_b[h, d, :, 0:flat] = pack_b(d)
+            copy_b(h, d, me).start()
+            return carry
+
+        lax.fori_loop(1, groups, start_b, 0)
+        recv_b[h, me, :, 0:flat] = pack_b(me)
+
+    for h in range(2):
+
+        def take_b(o, carry, h=h):
+            s = (me + groups - o) % groups
+            copy_b(h, s, s).wait_recv()
+            return carry
+
+        lax.fori_loop(1, groups, take_b, 0)
+
+    triangle = jnp.concatenate(
+        [recv_b[h, :, :, 0:flat].astype(jnp.float32) for h in range(2)], axis=1
+    ).reshape(hidden, flat)
     normed_tri = layer_norm_lead(triangle).astype(jnp.bfloat16)
     mixed = lax.dot_general(
         normed_tri, out_w_ref[...], (((0,), (0,)), ((), ())), preferred_element_type=jnp.float32
     )
     update = gate_f32[...] * mixed
     for j in range(cols):
-        rows_f32[pl.ds(j, rows, stride=pad), :] = update[j * rows : (j + 1) * rows]
-    for i in range(rows):
-        out_ref[i] = rows_f32[pl.ds(i * pad, cols), :].astype(jnp.bfloat16)
+        out_ref[j] = update[j * rows : (j + 1) * rows].astype(jnp.bfloat16)
 
     def finish(o, carry):
         d = (me + o) % groups
-        copy_a(d, me).wait_send()
-        copy_b(d, me).wait_send()
+        copy_r(d, me).wait_send()
+        for h in range(2):
+            copy_l(h, d, me).wait_send()
+            copy_b(h, d, me).wait_send()
         return carry
 
     lax.fori_loop(1, groups, finish, 0)
@@ -328,21 +362,22 @@
 def scratch_list(rows, cols, chans, hidden, groups, residues):
     gc = hidden // groups
     flat = up(rows * cols, LANES)
-    pad = up(cols, 8)
+    hc = gc // 2
     bf, f32 = jnp.bfloat16, jnp.float32
     return [
-        ((rows * pad, chans), f32),
         ((rows * cols, chans), bf),
         ((rows * cols, chans), bf),
         ((rows * cols, chans), f32),
-        ((groups, 2, gc, flat), bf),
-        ((groups, 2, gc, flat), bf),
         ((groups, gc, flat), bf),
+        ((groups, gc, flat), bf),
+        ((groups, gc, flat), bf),
+        ((2, groups, hc, flat), bf),
+        ((2, groups, hc, flat), bf),
         ((residues * gc, LANES), f32),
         ((2, residues * gc, LANES), f32),
         ((residues * gc, LANES), f32),
-        ((groups, gc, flat), bf),
-        ((groups, gc, flat), bf),
+        ((2, groups, hc, flat), bf),
+        ((2, groups, hc, flat), bf),
     ]
 
 
@@ -369,22 +404,28 @@
         return local(pair_map, residue_mask, proj_weight, gate_weight, out_weight)
     groups = sizes["gy"] * sizes["gz"]
     dma = pltpu.SemaphoreType.DMA((groups,))
+    dma_halves = pltpu.SemaphoreType.DMA((2, groups))
     vmem = pl.BlockSpec(memory_space=pltpu.VMEM)
-    return pl.pallas_call(
+    turned = pl.pallas_call(
         functools.partial(fused_kernel, sizes["gy"], sizes["gz"]),
-        out_shape=jax.ShapeDtypeStruct(pair_map.shape, jnp.bfloat16),
+        out_shape=jax.ShapeDtypeStruct((cols, rows, chans), jnp.bfloat16),
         in_specs=[vmem] * 5,
         out_specs=vmem,
         scratch_shapes=[
             pltpu.VMEM(shape, kind)
             for shape, kind in scratch_list(rows, cols, chans, hidden, groups, residues)
         ]
-        + [dma] * 6
-        + [pltpu.SemaphoreType.DMA((2,))],
+        + [dma] * 4
+        + [dma_halves] * 4
+        + [pltpu.SemaphoreType.DMA((1,))],
         compiler_params=pltpu.CompilerParams(
             collective_id=0, has_side_effects=True, vmem_limit_bytes=VMEM_BUDGET
         ),
-    )(pair_map, residue_mask.reshape(1, residues), proj_weight, gate_weight, out_weight)
+    )(
+        pair_map.transpose(1, 0, 2), residue_mask.reshape(1, residues),
+        proj_weight, gate_weight, out_weight,
+    )
+    return turned.transpose(1, 0, 2)
 
 
 def solution(mesh):

time: 31.2 us -> 35 us (1.12)
  local copies, waits for them, and re-layouts: 1.79 us -> 4.71 us
  Pallas kernels: 29.2 us -> 29.9 us
    unnamed x9 -> x11, local copies, waits for them, and re-layouts: 1.05 us -> 4.71 us
    pallas_call x1, Pallas kernels: 29.2 us -> 29.9 us  [local_fused(): pl.pallas_call(functools.partial(fused_kernel, sizes['gy'], sizes['gz']),...]
    pallas_call x1 -> x0, local copies, waits for them, and re-layouts: 0.73 us -> none  [local_fused(): pl.pallas_call(functools.partial(fused_kernel, sizes['gy'], sizes['gz']),...]
where the time goes in v2:
time: 35 us; the launch traced here: 34.7 us
  Pallas kernels  29.9 us (85%)
  local copies, waits for them, and re-layouts  4.71 us (13%)
    pallas_call x1, Pallas kernels, local_fused(): pl.pallas_call(functools.partial(fused_kernel, sizes['gy'], sizes['gz']),...  29.9 us
    unnamed x11, local copies, waits for them, and re-layouts  4.71 us

profile of v2, /device:TPU:0, one launch (start us, length us, event | category | flops | bytes accessed | tf_op | source)
XLA Modules:
  0.0 34.7 jit_solution(15371953256630785810)
XLA Ops:
  0.0 0.0 copy-start.4
  0.0 0.7 %copy-done.4 = s32[160]{0:T(256)S(1)} copy-done((s32[160]{0:T(256)S(1)}, s32[160]{0:T(256)}, u32[]{:S(2)}) %copy-start.4) | copy-done | bytes 664
  0.7 0.0 copy-start
  0.7 0.9 %copy-done = bf16[80,10,128]{2,0,1:T(8,128)(2,1)S(1)} copy-done((bf16[80,10,128]{2,0,1:T(8,128)(2,1)S(1)}, bf16[80,10,128]{2,0,1:T(8,128)(2,1)}, u32[]{:S(2)}) %copy-start) | copy-done | bytes 204824
  1.6 0.0 copy-start.1
  1.6 0.9 %copy-done.1 = bf16[128,512]{1,0:T(8,128)(2,1)S(1)} copy-done((bf16[128,512]{1,0:T(8,128)(2,1)S(1)}, bf16[128,512]{1,0:T(8,128)(2,1)}, u32[]{:S(2)}) %copy-start.1) | copy-done | bytes 131096
  2.5 0.0 copy-start.2
  2.5 0.8 %copy-done.2 = bf16[128,128]{1,0:T(8,128)(2,1)S(1)} copy-done((bf16[128,128]{1,0:T(8,128)(2,1)S(1)}, bf16[128,128]{1,0:T(8,128)(2,1)}, u32[]{:S(2)}) %copy-start.2) | copy-done | bytes 32792
  3.3 0.0 copy-start.3
  3.3 0.8 %copy-done.3 = bf16[128,128]{1,0:T(8,128)(2,1)S(1)} copy-done((bf16[128,128]{1,0:T(8,128)(2,1)S(1)}, bf16[128,128]{1,0:T(8,128)(2,1)}, u32[]{:S(2)}) %copy-start.3) | copy-done | bytes 32792
  4.0 29.9 %shard_map.55 = bf16[10,80,128]{2,1,0:T(8,128)(2,1)S(1)} custom-call(bf16[10,80,128]{2,1,0:T(8,128)(2,1)S(1)} %bitcast.4, s32[1,160]{1,0:T(1,128)S(1)} %bitcast.5, bf16[128,512]{1,0:T(8,128)(2,1)S(1)} %copy-done.1, bf16[128,128]{1,0:T(8,128)(2,1)S(1)} %copy-done.2, bf16[128,128]{1,0:T(8,128)(2,1)S(1)} %copy-done.3), custom_call_target="tpu_custom_call" | custom-call | tf_op jit(solution)/shard_map/pallas_call | solution.py:409
  34.0 0.7 %copy.7 = bf16[80,10,128]{2,0,1:T(8,128)(2,1)} copy(bf16[80,10,128]{2,0,1:T(8,128)(2,1)S(1)} %bitcast.3) | data formatting | bytes 409600
Async XLA Ops:
  0.0 0.7 %copy-start.4 = (s32[160]{0:T(256)S(1)}, s32[160]{0:T(256)}, u32[]{:S(2)}) copy-start(s32[160]{0:T(256)} %param.6) | copy-start | bytes 1924
  0.7 0.9 %copy-start = (bf16[80,10,128]{2,0,1:T(8,128)(2,1)S(1)}, bf16[80,10,128]{2,0,1:T(8,128)(2,1)}, u32[]{:S(2)}) copy-start(bf16[80,10,128]{2,0,1:T(8,128)(2,1)} %param.5) | copy-start | bytes 614404
  1.6 0.9 %copy-start.1 = (bf16[128,512]{1,0:T(8,128)(2,1)S(1)}, bf16[128,512]{1,0:T(8,128)(2,1)}, u32[]{:S(2)}) copy-start(bf16[128,512]{1,0:T(8,128)(2,1)} %proj_ref.1) | copy-start | bytes 393220
  2.5 0.8 %copy-start.2 = (bf16[128,128]{1,0:T(8,128)(2,1)S(1)}, bf16[128,128]{1,0:T(8,128)(2,1)}, u32[]{:S(2)}) copy-start(bf16[128,128]{1,0:T(8,128)(2,1)} %gate_ref.1) | copy-start | bytes 98308
  3.3 0.8 %copy-start.3 = (bf16[128,128]{1,0:T(8,128)(2,1)S(1)}, bf16[128,128]{1,0:T(8,128)(2,1)}, u32[]{:S(2)}) copy-start(bf16[128,128]{1,0:T(8,128)(2,1)} %out_w_ref.1) | copy-start | bytes 98308

commit v3 on v2

--- a/solution.py
+++ b/solution.py
@@ -130,6 +130,7 @@
 
 MESH = pl.DeviceIdType.MESH
 LANES = 128
+PIECES = 1
 VMEM_BUDGET = 48 * 2**20
 
 
@@ -148,7 +149,7 @@
     hidden = out_w_ref.shape[0]
     groups = along_y * along_z
     gc = hidden // groups
-    hc = gc // 2
+    hc = gc // PIECES
     flat = rows * cols
     residues = mask_ref.shape[1]
     px, py, pz = lax.axis_index("gx"), lax.axis_index("gy"), lax.axis_index("gz")
@@ -241,11 +242,11 @@
     for first in range(0, hidden, step):
         value = gated(first, 0)
         for part in range(step // gc):
-            for h in range(2):
+            for h in range(PIECES):
                 low = part * gc + h * hc
                 send_l[h, first // gc + part, :, 0:flat] = value[low : low + hc].astype(jnp.bfloat16)
 
-    for h in range(2):
+    for h in range(PIECES):
 
         def start_l(o, carry, h=h):
             copy_l(h, (me + o) % groups, me).start()
@@ -286,7 +287,7 @@
 
     lax.fori_loop(0, groups, take_x, 0)
 
-    for h in range(2):
+    for h in range(PIECES):
         spread(send_l[h, me], left_s, me, h * hc, hc)
 
         def take_l(o, carry, h=h):
@@ -322,7 +323,7 @@
         lax.fori_loop(1, groups, start_b, 0)
         recv_b[h, me, :, 0:flat] = pack_b(me)
 
-    for h in range(2):
+    for h in range(PIECES):
 
         def take_b(o, carry, h=h):
             s = (me + groups - o) % groups
@@ -332,7 +333,7 @@
         lax.fori_loop(1, groups, take_b, 0)
 
     triangle = jnp.concatenate(
-        [recv_b[h, :, :, 0:flat].astype(jnp.float32) for h in range(2)], axis=1
+        [recv_b[h, :, :, 0:flat].astype(jnp.float32) for h in range(PIECES)], axis=1
     ).reshape(hidden, flat)
     normed_tri = layer_norm_lead(triangle).astype(jnp.bfloat16)
     mixed = lax.dot_general(
@@ -345,7 +346,7 @@
     def finish(o, carry):
         d = (me + o) % groups
         copy_r(d, me).wait_send()
-        for h in range(2):
+        for h in range(PIECES):
             copy_l(h, d, me).wait_send()
             copy_b(h, d, me).wait_send()
         return carry
@@ -362,7 +363,7 @@
 def scratch_list(rows, cols, chans, hidden, groups, residues):
     gc = hidden // groups
     flat = up(rows * cols, LANES)
-    hc = gc // 2
+    hc = gc // PIECES
     bf, f32 = jnp.bfloat16, jnp.float32
     return [
         ((rows * cols, chans), bf),
@@ -371,13 +372,13 @@
         ((groups, gc, flat), bf),
         ((groups, gc, flat), bf),
         ((groups, gc, flat), bf),
-        ((2, groups, hc, flat), bf),
-        ((2, groups, hc, flat), bf),
+        ((PIECES, groups, hc, flat), bf),
+        ((PIECES, groups, hc, flat), bf),
         ((residues * gc, LANES), f32),
         ((2, residues * gc, LANES), f32),
         ((residues * gc, LANES), f32),
-        ((2, groups, hc, flat), bf),
-        ((2, groups, hc, flat), bf),
+        ((PIECES, groups, hc, flat), bf),
+        ((PIECES, groups, hc, flat), bf),
     ]
 
 
@@ -404,7 +405,7 @@
         return local(pair_map, residue_mask, proj_weight, gate_weight, out_weight)
     groups = sizes["gy"] * sizes["gz"]
     dma = pltpu.SemaphoreType.DMA((groups,))
-    dma_halves = pltpu.SemaphoreType.DMA((2, groups))
+    dma_halves = pltpu.SemaphoreType.DMA((PIECES, groups))
     vmem = pl.BlockSpec(memory_space=pltpu.VMEM)
     turned = pl.pallas_call(
         functools.partial(fused_kernel, sizes["gy"], sizes["gz"]),

time: 35 us -> 31.1 us (0.89)
  Pallas kernels: 29.9 us -> 26 us
    pallas_call x1, Pallas kernels: 29.9 us -> 26 us  [local_fused(): pl.pallas_call(functools.partial(fused_kernel, sizes['gy'], sizes['gz']),...]
where the time goes in v3:
time: 31.1 us; the launch traced here: 30.8 us
  Pallas kernels  26 us (84%)
  local copies, waits for them, and re-layouts  4.71 us (15%)
    pallas_call x1, Pallas kernels, local_fused(): pl.pallas_call(functools.partial(fused_kernel, sizes['gy'], sizes['gz']),...  26 us
    unnamed x11, local copies, waits for them, and re-layouts  4.71 us

profile of v3, /device:TPU:0, one launch (start us, length us, event | category | flops | bytes accessed | tf_op | source)
XLA Modules:
  0.0 30.8 jit_solution(16785970381430018211)
XLA Ops:
  0.0 0.0 copy-start.4
  0.0 0.7 %copy-done.4 = s32[160]{0:T(256)S(1)} copy-done((s32[160]{0:T(256)S(1)}, s32[160]{0:T(256)}, u32[]{:S(2)}) %copy-start.4) | copy-done | bytes 664
  0.7 0.0 copy-start
  0.7 0.9 %copy-done = bf16[80,10,128]{2,0,1:T(8,128)(2,1)S(1)} copy-done((bf16[80,10,128]{2,0,1:T(8,128)(2,1)S(1)}, bf16[80,10,128]{2,0,1:T(8,128)(2,1)}, u32[]{:S(2)}) %copy-start) | copy-done | bytes 204824
  1.6 0.0 copy-start.1
  1.6 0.9 %copy-done.1 = bf16[128,512]{1,0:T(8,128)(2,1)S(1)} copy-done((bf16[128,512]{1,0:T(8,128)(2,1)S(1)}, bf16[128,512]{1,0:T(8,128)(2,1)}, u32[]{:S(2)}) %copy-start.1) | copy-done | bytes 131096
  2.5 0.0 copy-start.2
  2.5 0.8 %copy-done.2 = bf16[128,128]{1,0:T(8,128)(2,1)S(1)} copy-done((bf16[128,128]{1,0:T(8,128)(2,1)S(1)}, bf16[128,128]{1,0:T(8,128)(2,1)}, u32[]{:S(2)}) %copy-start.2) | copy-done | bytes 32792
  3.3 0.0 copy-start.3
  3.3 0.8 %copy-done.3 = bf16[128,128]{1,0:T(8,128)(2,1)S(1)} copy-done((bf16[128,128]{1,0:T(8,128)(2,1)S(1)}, bf16[128,128]{1,0:T(8,128)(2,1)}, u32[]{:S(2)}) %copy-start.3) | copy-done | bytes 32792
  4.0 26.0 %shard_map.55 = bf16[10,80,128]{2,1,0:T(8,128)(2,1)S(1)} custom-call(bf16[10,80,128]{2,1,0:T(8,128)(2,1)S(1)} %bitcast.4, s32[1,160]{1,0:T(1,128)S(1)} %bitcast.5, bf16[128,512]{1,0:T(8,128)(2,1)S(1)} %copy-done.1, bf16[128,128]{1,0:T(8,128)(2,1)S(1)} %copy-done.2, bf16[128,128]{1,0:T(8,128)(2,1)S(1)} %copy-done.3), custom_call_target="tpu_custom_call" | custom-call | tf_op jit(solution)/shard_map/pallas_call | solution.py:410
  30.1 0.7 %copy.7 = bf16[80,10,128]{2,0,1:T(8,128)(2,1)} copy(bf16[80,10,128]{2,0,1:T(8,128)(2,1)S(1)} %bitcast.3) | data formatting | bytes 409600
Async XLA Ops:
  0.0 0.7 %copy-start.4 = (s32[160]{0:T(256)S(1)}, s32[160]{0:T(256)}, u32[]{:S(2)}) copy-start(s32[160]{0:T(256)} %param.6) | copy-start | bytes 1924
  0.7 0.9 %copy-start = (bf16[80,10,128]{2,0,1:T(8,128)(2,1)S(1)}, bf16[80,10,128]{2,0,1:T(8,128)(2,1)}, u32[]{:S(2)}) copy-start(bf16[80,10,128]{2,0,1:T(8,128)(2,1)} %param.5) | copy-start | bytes 614404
  1.6 0.9 %copy-start.1 = (bf16[128,512]{1,0:T(8,128)(2,1)S(1)}, bf16[128,512]{1,0:T(8,128)(2,1)}, u32[]{:S(2)}) copy-start(bf16[128,512]{1,0:T(8,128)(2,1)} %proj_ref.1) | copy-start | bytes 393220
  2.5 0.8 %copy-start.2 = (bf16[128,128]{1,0:T(8,128)(2,1)S(1)}, bf16[128,128]{1,0:T(8,128)(2,1)}, u32[]{:S(2)}) copy-start(bf16[128,128]{1,0:T(8,128)(2,1)} %gate_ref.1) | copy-start | bytes 98308
  3.3 0.8 %copy-start.3 = (bf16[128,128]{1,0:T(8,128)(2,1)S(1)}, bf16[128,128]{1,0:T(8,128)(2,1)}, u32[]{:S(2)}) copy-start(bf16[128,128]{1,0:T(8,128)(2,1)} %out_w_ref.1) | copy-start | bytes 98308

commit v4 on v3

--- a/solution.py
+++ b/solution.py
@@ -131,6 +131,7 @@
 MESH = pl.DeviceIdType.MESH
 LANES = 128
 PIECES = 1
+VMEM_GRANT = 67043328
 VMEM_BUDGET = 48 * 2**20
 
 
@@ -140,10 +141,11 @@
 
 def fused_kernel(
     along_y, along_z,
-    pair_ref, mask_ref, proj_ref, gate_ref, out_w_ref, out_ref,
+    pair_hbm, mask_hbm, proj_hbm, gate_hbm, out_w_hbm, out_ref,
+    pair_ref, mask_ref, proj_ref, gate_ref, out_w_ref,
     normed_bf, masked_bf, gate_f32, send_r, recv_r, recv_x, send_l, recv_l,
     left_s, right_s, tri_s, send_b, recv_b,
-    ssem_r, rsem_r, ssem_x, rsem_x, ssem_l, rsem_l, ssem_b, rsem_b, own_sem,
+    ssem_r, rsem_r, ssem_x, rsem_x, ssem_l, rsem_l, ssem_b, rsem_b, own_sem, load_sem,
 ):
     cols, rows, chans = pair_ref.shape
     hidden = out_w_ref.shape[0]
@@ -168,6 +170,20 @@
     lax.fori_loop(1, groups, greet, 0)
     pl.semaphore_signal(barrier, inc=1, device_id=partner, device_id_type=MESH)
 
+    loads = [
+        pltpu.make_async_copy(source, target, load_sem.at[n])
+        for n, (source, target) in enumerate(
+            (
+                (pair_hbm, pair_ref), (mask_hbm, mask_ref), (proj_hbm, proj_ref),
+                (gate_hbm, gate_ref), (out_w_hbm, out_w_ref),
+            )
+        )
+    ]
+    for load in loads:
+        load.start()
+    loads[0].wait()
+    loads[1].wait()
+
     mask_f = mask_ref[...].astype(jnp.float32)
     lane = lax.broadcasted_iota(jnp.int32, (rows, residues), 1)
     sub = lax.broadcasted_iota(jnp.int32, (rows, residues), 0)
@@ -183,6 +199,7 @@
             normed.astype(jnp.float32) * (row_mask * col_mask)
         ).astype(jnp.bfloat16)
 
+    loads[2].wait()
     proj_t = proj_ref[...].astype(jnp.float32).T.astype(jnp.bfloat16)
     masked = masked_bf[...]
 
@@ -254,6 +271,8 @@
 
         lax.fori_loop(1, groups, start_l, 0)
 
+    loads[3].wait()
+    loads[4].wait()
     gate_f32[...] = jax.nn.sigmoid(
         jnp.dot(normed_bf[...], gate_ref[...], preferred_element_type=jnp.float32)
     )
@@ -366,6 +385,11 @@
     hc = gc // PIECES
     bf, f32 = jnp.bfloat16, jnp.float32
     return [
+        ((cols, rows, chans), bf),
+        ((1, residues), jnp.int32),
+        ((chans, 4 * hidden), bf),
+        ((chans, chans), bf),
+        ((hidden, chans), bf),
         ((rows * cols, chans), bf),
         ((rows * cols, chans), bf),
         ((rows * cols, chans), f32),
@@ -410,7 +434,7 @@
     turned = pl.pallas_call(
         functools.partial(fused_kernel, sizes["gy"], sizes["gz"]),
         out_shape=jax.ShapeDtypeStruct((cols, rows, chans), jnp.bfloat16),
-        in_specs=[vmem] * 5,
+        in_specs=[pl.BlockSpec(memory_space=pltpu.HBM)] * 5,
         out_specs=vmem,
         scratch_shapes=[
             pltpu.VMEM(shape, kind)
@@ -418,9 +442,9 @@
         ]
         + [dma] * 4
         + [dma_halves] * 4
-        + [pltpu.SemaphoreType.DMA((1,))],
+        + [pltpu.SemaphoreType.DMA((1,)), pltpu.SemaphoreType.DMA((5,))],
         compiler_params=pltpu.CompilerParams(
-            collective_id=0, has_side_effects=True, vmem_limit_bytes=VMEM_BUDGET
+            collective_id=0, has_side_effects=True, vmem_limit_bytes=VMEM_GRANT
         ),
     )(
         pair_map.transpose(1, 0, 2), residue_mask.reshape(1, residues),

time: 31.1 us -> 29.4 us (0.945)
  local copies, waits for them, and re-layouts: 4.71 us -> 1.62 us
  Pallas kernels: 26 us -> 27.6 us
    unnamed x11 -> x1, local copies, waits for them, and re-layouts: 4.71 us -> 1.62 us
    pallas_call x1, Pallas kernels: 26 us -> 27.6 us  [local_fused(): pl.pallas_call(functools.partial(fused_kernel, sizes['gy'], sizes['gz']),...]
where the time goes in v4:
time: 29.4 us; the launch traced here: 29.3 us
  Pallas kernels  27.6 us (94%)
  local copies, waits for them, and re-layouts  1.62 us (6%)
    pallas_call x1, Pallas kernels, local_fused(): pl.pallas_call(functools.partial(fused_kernel, sizes['gy'], sizes['gz']),...  27.6 us
    unnamed x1, local copies, waits for them, and re-layouts  1.62 us

profile of v4, /device:TPU:0, one launch (start us, length us, event | category | flops | bytes accessed | tf_op | source)
XLA Modules:
  0.0 29.3 jit_solution(10142544383507697276)
XLA Ops:
  0.0 27.6 %shard_map.55 = bf16[10,80,128]{2,1,0:T(8,128)(2,1)} custom-call(bf16[10,80,128]{2,1,0:T(8,128)(2,1)} %bitcast.4, s32[1,160]{1,0:T(1,128)} %bitcast.5, bf16[128,512]{1,0:T(8,128)(2,1)} %proj_hbm.1, bf16[128,128]{1,0:T(8,128)(2,1)} %gate_hbm.1, bf16[128,128]{1,0:T(8,128)(2,1)} %out_w_hbm.1), custom_call_target="tpu_custom_call" | custom-call | tf_op jit(solution)/shard_map/pallas_call | solution.py:434
  27.6 1.6 %copy.7 = bf16[80,10,128]{2,0,1:T(8,128)(2,1)} copy(bf16[80,10,128]{2,0,1:T(8,128)(2,1)} %bitcast.3) | data formatting | bytes 409600
